TPU v7x, 32 devices: a whole 2x2x4 slice. The times are simulated.
32 devices in a mesh: vocab: 8 (over z, y), batch: 4 (over x, core).
Axes of the slice: x: 2, y: 2, z: 4, core: 2. Of those that a mesh axis runs over, the one named last changes fastest.
Arguments:
- latent_state_rows: bfloat16 [64, 8192], P('batch', 'vocab'), may hold values from -90 to 90
- closing_rescale_coeffs: bfloat16 [8192], replicated, may hold values from 0.5 to 1.5
- output_projection_matrix: bfloat16 [8192, 131072], P(None, ('vocab', 'batch')), may hold values from -3.7565048 to 3.7565048
- config_heat_values: float32 [16], replicated, may hold values from 0.7 to 1.4
- sequence_config_choice: int32 [64], replicated, may hold values from 0 to 15
- ranked_choice_ids: int32 [64, 128], replicated, may hold values from 0 to 131071
- keep_count: int32 [64], replicated, may hold values from 2 to 128
Outputs:
- log_norm: float32 [64], P('batch')
- kept_mass: float32 [64], P('batch')
- renormed: float32 [64, 128], P('batch')
All inputs are finite; a program needn't handle non-finite values.
Results may differ from a plain program's by a relative error of at most 0.0048.
Values may be sent and summed in bfloat16 or wider, within the bound.
No kernel may reach another device: no remote copies, remote signals or barrier semaphores. Data moves between devices by JAX's collectives and lax.ppermute only.
A program may use at most 128 MiB of HBM per device.

v0:
```python
import jax
import jax.numpy as jnp
from jax import lax
from jax.sharding import PartitionSpec as P

epsilon = 1e-06


def normalize(values, gain_part, mean_square):
    factor = lax.rsqrt(mean_square + epsilon)
    return (values * factor[:, None] * gain_part[None, :]).astype(jnp.bfloat16)


def rows_normed(raw_rows, gain_full):
    values = raw_rows.astype(jnp.float32)
    return normalize(values, gain_full, jnp.mean(values * values, axis=1))


def local(
    latent_state_rows,
    closing_rescale_coeffs,
    output_projection_matrix,
    config_heat_values,
    sequence_config_choice,
    ranked_choice_ids,
    keep_count,
):
    group_rows = latent_state_rows.shape[0]
    col_count = output_projection_matrix.shape[1]
    batch_count = lax.axis_size("batch")
    vocab_pos = lax.axis_index("vocab")
    batch_pos = lax.axis_index("batch")
    gain_full = closing_rescale_coeffs.astype(jnp.float32)
    wide_rows = lax.all_gather(latent_state_rows, "vocab", axis=1, tiled=True)
    unnormalized_scores = jnp.dot(
        rows_normed(lax.all_gather(wide_rows, "batch", axis=0, tiled=True), gain_full),
        output_projection_matrix,
        preferred_element_type=jnp.float32,
    )
    config_membership = (
        sequence_config_choice[:, None]
        == jnp.arange(config_heat_values.shape[0], dtype=jnp.int32)[None, :]
    ).astype(jnp.float32)
    sequence_heat_values = jnp.sum(config_membership * config_heat_values[None, :], axis=1)
    divided_scores = unnormalized_scores / sequence_heat_values[:, None]
    offset = (vocab_pos * batch_count + batch_pos) * col_count
    local_ids = ranked_choice_ids - offset
    owned = (local_ids >= 0) & (local_ids < col_count)
    picked = jnp.take_along_axis(divided_scores, jnp.clip(local_ids, 0, col_count - 1), axis=1)
    cand_local = jnp.where(owned, picked, jnp.float32(0.0))
    local_top = jnp.max(divided_scores, axis=1)
    first_slot = batch_pos * group_rows
    row_top = lax.pmax(local_top, ("vocab", "batch"))
    row_total = lax.psum(
        jnp.sum(jnp.exp(divided_scores - row_top[:, None]), axis=1), ("vocab", "batch")
    )
    cand_logit = lax.psum(cand_local, ("vocab", "batch"))
    own_top = lax.dynamic_slice_in_dim(row_top, first_slot, group_rows)
    own_total = lax.dynamic_slice_in_dim(row_total, first_slot, group_rows)
    own_cand = lax.dynamic_slice_in_dim(cand_logit, first_slot, group_rows, 0)
    own_cutoff = lax.dynamic_slice_in_dim(keep_count, first_slot, group_rows)
    log_norm = own_top + jnp.log(own_total)
    kept_mask = jnp.arange(own_cand.shape[1], dtype=jnp.int32)[None, :] < own_cutoff[:, None]
    kept_top = jnp.max(jnp.where(kept_mask, own_cand, jnp.float32(-3e38)), axis=1)
    shifted = jnp.where(kept_mask, own_cand - kept_top[:, None], jnp.float32(0.0))
    kept_exp = jnp.where(kept_mask, jnp.exp(shifted), jnp.float32(0.0))
    kept_sum = jnp.sum(kept_exp, axis=1)
    kept_mass = kept_top + jnp.log(kept_sum) - log_norm
    return (log_norm, kept_mass, kept_exp / kept_sum[:, None])


def solution(mesh):
    placed = (P("batch", "vocab"), P(), P(None, ("vocab", "batch")), P(), P(), P(), P())
    return jax.shard_map(
        local,
        mesh=mesh,
        in_specs=placed,
        out_specs=(P("batch"), P("batch"), P("batch", None)),
        check_vma=False,
    )
```

profile of v0, /device:TPU:0, one launch (start us, length us, event | category | flops | bytes accessed | tf_op | source)
XLA Modules:
  0.0 239.7 jit_solution(4070689631893379016)
XLA Ops:
  7.2 0.0 all-gather.2.cloned.1.call-start
  7.2 34.8 %all_gather.6 = bf16[16,8192]{1,0:T(8,128)(2,1)} all-gather(bf16[16,1024]{1,0:T(8,128)(2,1)} %param.7), channel_id=1, replica_groups=mesh['vocab'=8,'batch'=4] {'vocab'}, dimensions={1}, use_global_device_ids=true | all-gather | bytes 294912 | tf_op jit(solution)/shard_map/all_gather | solution.py:34
  42.0 0.0 all-gather.2.cloned.1.call-update
  42.0 0.7 convert_element_type.11
  42.7 0.7 dynamic_slice.14
  43.5 0.8 select_reduce_fusion.1
  44.2 0.8 fusion.7
  45.0 14.8 %all-gather.2.cloned.1.call-done = bf16[64,8192]{1,0:T(8,128)(2,1)} async-done(((bf16[16,8192]{1,0:T(8,128)(2,1)}), bf16[64,8192]{1,0:T(8,128)(2,1)}) %all-gather.2.cloned.1.call-update) | async-done | bytes 1048592 | tf_op jit(solution)/shard_map/all_gather | solution.py:36
  59.8 1.5 fusion
  61.3 23.9 %fusion.10 = (f32[64]{0:T(128)S(1)}, f32[64,4096]{1,0:T(8,128)S(1)}) fusion(f32[64]{0:T(128)S(1)} %select_reduce_fusion.1, bf16[8192,4096]{1,0:T(8,128)(2,1)} %param.9, bf16[64,8192]{1,0:T(8,128)(2,1)} %all-gather.2.cloned.1.call-done, f32[8192]{0:T(1024)S(1)} %convert_element_type.11, f32[64]{0:T(128)S(1)} %add_rsqrt_fusion), kind=kOutput, calls=%fused_computation.25 | convolution fusion | flops 4297588736 | bytes 69239552 | tf_op jit(solution)/shard_map/dot_general | solution.py:35
  85.2 0.0 copy-start
  85.2 65.0 %gather_fusion = f32[8192]{0:T(1024)S(1)} fusion(f32[64,4096]{1,0:T(8,128)S(1)} %get-tuple-element.8, s32[8192]{0:T(1024)S(1)} %fusion.7), kind=kCustom, calls=%fused_computation | custom fusion | bytes 131072 | tf_op jit(solution)/shard_map/jit(take_along_axis)/gather | solution.py:49
  150.3 0.0 copy-done
  150.3 39.3 %pmax.7 = f32[64]{0:T(128)S(1)} all-reduce(f32[64]{0:T(128)S(1)} %get-tuple-element.7), channel_id=1, replica_groups=mesh['vocab'=8,'batch'=4] {'vocab','batch'}, use_global_device_ids=true, to_apply=%region_3.4 | all-reduce | flops 64 | bytes 512 | tf_op jit(solution)/shard_map/pmax | solution.py:53
  189.6 0.3 exponential_reduce_fusion
  189.9 41.3 %all-reduce = (f32[64]{0:T(128)S(1)}, f32[64,128]{1,0:T(8,128)S(1)}) all-reduce(f32[64]{0:T(128)S(1)} %exponential_reduce_fusion, f32[64,128]{1,0:T(8,128)S(1)} %fusion.6), channel_id=1, replica_groups=mesh['vocab'=8,'batch'=4] {'vocab','batch'}, use_global_device_ids=true, to_apply=%region_5.6 | all-reduce | flops 8256 | bytes 66048 | tf_op jit(solution)/shard_map/psum | solution.py:54
  231.2 0.2 select_reduce_fusion
  231.4 0.2 fusion.9
  231.6 0.7 fusion.8
  232.3 0.6 add_subtract_fusion
  (2 shorter events, 0.0 us)
Async XLA Ops:
  7.2 52.6 %all-gather.2.cloned.1.call-start = ((), (), s32[]{:S(2)}) async-start(), calls=%async_computation | async-start | bytes 1310720 | tf_op jit(solution)/shard_map/all_gather | solution.py:36
  85.2 65.0 %copy-start = (s32[64,128]{1,0:T(8,128)S(1)}, s32[64,128]{1,0:T(8,128)}, u32[]{:S(2)}) copy-start(s32[64,128]{1,0:T(8,128)} %param.12) | copy-start | bytes 98308
Sparse Core Ops, SparseCore 0:
  42.1 17.5 all-gather.1
where the time goes:
time: 240 us
  blocking collectives  115 us (48%)
  local copies, waits for them, and re-layouts  65.7 us (27%)
  matrix products  23.9 us (10%)
  waiting for transfers between devices  14.8 us (6%)
  between operations  14.1 us (6%)
  other arithmetic  5.8 us (2%)
    gather x1, local copies, waits for them, and re-layouts, local(): jnp.take_along_axis(divided_scores, jnp.clip(local_ids, 0, col_count - 1)...  65 us
    psum x1, blocking collectives, local(): lax.psum(jnp.sum(jnp.exp(divided_scores - row_top[:, None]), axis=1), ('v...  41.3 us
    pmax x1, blocking collectives, local(): row_top = lax.pmax(local_top, ('vocab', 'batch'))  39.3 us
    all_gather x1, blocking collectives, local(): wide_rows = lax.all_gather(latent_state_rows, 'vocab', axis=1, tiled=True)  34.8 us
    dot_general x1, matrix products, local(): jnp.dot(rows_normed(lax.all_gather(wide_rows, 'batch', axis=0, tiled=True...  23.9 us
    all_gather x1, waiting for transfers between devices, local(): lax.all_gather(wide_rows, 'batch', axis=0, tiled=True)  14.8 us
  transfers between devices with their start and end apart: 1, of which 1 were waited for; matrix products, arithmetic and copies ran while one was open for 1% of the time, Pallas kernels for 0%

commit v1 on v0

v1 whole, which is shorter than its diff:
```python
import functools

import jax
import jax.numpy as jnp
from jax import lax
from jax.experimental import pallas as pl
from jax.experimental.pallas import tpu as pltpu
from jax.sharding import PartitionSpec as P


epsilon = 1e-06
LANES = 128
UNITS = 32
CHUNKS = 2
EARLY_UNITS = (6, 4, 5, 1)
BESIDE_UNITS = 6
MIB = 1 << 20
SLAB = 1024


VMEM = pl.BlockSpec(memory_space=pltpu.VMEM)
SMEM = pl.BlockSpec(memory_space=pltpu.SMEM)
ANY = pl.BlockSpec(memory_space=pl.ANY)


def bits_of(count):
    return [1 << n for n in range(count.bit_length() - 1)]


def swap(value, axis, bit):
    count = lax.axis_size(axis)
    return lax.ppermute(value, axis, [(n, n ^ bit) for n in range(count)])


def swap_both(value, vocab_offset, batch_offset):
    vocab_count = lax.axis_size("vocab")
    batch_count = lax.axis_size("batch")
    pairs = [
        (v * batch_count + b, (v ^ vocab_offset) * batch_count + (b ^ batch_offset))
        for v in range(vocab_count)
        for b in range(batch_count)
    ]
    return lax.ppermute(value, ("vocab", "batch"), pairs)


def rounds_of(bits):
    bits = sorted(bits, reverse=True)
    return [bits[n : n + 2] for n in range(0, len(bits), 2)]


def offsets_of(bits):
    offsets = [0]
    for bit in bits:
        offsets += [offset ^ bit for offset in offsets]
    return offsets


def unit_copies(span, matrix_ref, target_ref, sems):
    first, count = span
    height = target_ref.shape[0] // count
    return [
        pltpu.make_async_copy(
            matrix_ref.at[pl.ds((first + n) * height, height)],
            target_ref.at[pl.ds(n * height, height)],
            sems.at[n],
        )
        for n in range(count)
    ]


def fetch_kernel(*refs, span):
    matrix_ref, out_ref, sems = refs[-3:]
    copies = unit_copies(span, matrix_ref, out_ref, sems)
    for copy in copies:
        copy.start()
    for copy in copies:
        copy.wait()


def rows_shape(span, matrix):
    features, cols = matrix.shape
    return pltpu.VMEM((features // UNITS * span[1], cols), matrix.dtype)


def fetch(span, matrix, after=None):
    operands = [matrix] if after is None else [after, matrix]
    return pl.pallas_call(
        functools.partial(fetch_kernel, span=span),
        out_shape=rows_shape(span, matrix),
        in_specs=[ANY] * len(operands),
        out_specs=VMEM,
        scratch_shapes=[pltpu.SemaphoreType.DMA((span[1],))],
        compiler_params=pltpu.CompilerParams(vmem_limit_bytes=MIB),
        cost_estimate=pl.CostEstimate(
            flops=span[1] * 10**10, bytes_accessed=matrix.size * 2 // UNITS * span[1], transcendentals=0
        ),
    )(*operands)


def norm_kernel(pieces_ref, gain_ref, *out_refs, offsets):
    vocab_pos = lax.axis_index("vocab")
    count, group_rows, part = pieces_ref.shape
    per_chunk = count // CHUNKS
    order_bits = [offsets[1 << n] for n in range(count.bit_length() - 1)]
    square = jnp.zeros((group_rows, part), jnp.float32)
    for n in range(count):
        values = pieces_ref[n].astype(jnp.float32)
        square = square + values * values
    factor = lax.rsqrt(jnp.sum(square, axis=1, keepdims=True) / (count * part) + epsilon)
    for n in range(count):
        apart = vocab_pos ^ n
        place = sum(
            ((apart >> (bit.bit_length() - 1)) & 1) << k for k, bit in enumerate(order_bits)
        )
        values = pieces_ref[place].astype(jnp.float32)
        gain = gain_ref[n * part : (n + 1) * part].astype(jnp.float32).reshape(1, part)
        out_refs[n // per_chunk][0, :, pl.ds(n % per_chunk * part, part)] = (
            values * factor * gain
        ).astype(jnp.bfloat16)


def norm(pieces, gain, offsets):
    count, group_rows, part = pieces.shape
    chunk = jax.ShapeDtypeStruct((1, group_rows, count * part // CHUNKS), jnp.bfloat16)
    return pl.pallas_call(
        functools.partial(norm_kernel, offsets=offsets),
        out_shape=(chunk,) * CHUNKS,
        in_specs=[VMEM, VMEM],
        out_specs=(VMEM,) * CHUNKS,
        compiler_params=pltpu.CompilerParams(vmem_limit_bytes=4 * MIB),
        name="norm",
    )(pieces, gain)


def product(rows_ref, chunk, weight_ref, span, cols, total=None):
    groups, group_rows, width = rows_ref.shape
    per_chunk = UNITS // CHUNKS
    unit = width // per_chunk
    low = max(span[0], chunk * per_chunk)
    high = min(span[0] + span[1], (chunk + 1) * per_chunk)
    if low >= high:
        return total
    rows = rows_ref[
        :, :, (low - chunk * per_chunk) * unit : (high - chunk * per_chunk) * unit
    ].reshape(groups * group_rows, (high - low) * unit)
    weights = weight_ref[(low - span[0]) * unit : (high - span[0]) * unit, cols]
    term = jnp.dot(rows, weights, preferred_element_type=jnp.float32)
    return term if total is None else total + term


def slab_copy(span, n, matrix_ref, target_ref, sems):
    _, height, width = target_ref.shape
    unit = height // span[1]
    return pltpu.make_async_copy(
        matrix_ref.at[
            pl.ds(span[0] * unit, height),
            pl.ds(n * width if isinstance(n, int) else pl.multiple_of(n * width, width), width),
        ],
        target_ref.at[n],
        sems.at[n],
    )


def slab_scores(n, rows_ref, chunk, parts, stream, matrix_ref, stream_ref, sems, total):
    width = stream_ref.shape[2]
    start = n * width if isinstance(n, int) else pl.multiple_of(n * width, width)
    cols = pl.ds(start, width)
    if not isinstance(n, int):
        slab_copy(stream, n, matrix_ref, stream_ref, sems).wait()
    for weight_ref, span in parts:
        total = product(rows_ref, chunk, weight_ref, span, cols, total)
    if isinstance(n, int):
        slab_copy(stream, n, matrix_ref, stream_ref, sems).wait()
    return product(rows_ref, chunk, stream_ref.at[n], stream, slice(None), total)


def partial_kernel(rows_ref, *refs, spans, beside):
    weight_refs, refs = refs[: len(spans)], refs[len(spans) :]
    matrix_ref, out_ref, fetched_ref, sems = refs
    copies = unit_copies(beside, matrix_ref, fetched_ref, sems)
    for copy in copies:
        copy.start()
    width = min(SLAB, out_ref.shape[1])

    def step(n, carry):
        cols = pl.ds(pl.multiple_of(n * width, width), width)
        total = None
        for weight_ref, span in zip(weight_refs, spans):
            total = product(rows_ref, 0, weight_ref, span, cols, total)
        out_ref[:, cols] = total
        return carry

    lax.fori_loop(0, out_ref.shape[1] // width, step, 0)
    for copy in copies:
        copy.wait()


def slabs_shape(span, matrix, width):
    features, cols = matrix.shape
    width = min(width, cols)
    return pltpu.VMEM((cols // width, features // UNITS * span[1], width), matrix.dtype)


def partial_scores(rows, weights, spans, matrix, beside):
    groups, group_rows, _ = rows.shape
    return pl.pallas_call(
        functools.partial(partial_kernel, spans=spans, beside=beside),
        out_shape=(
            pltpu.VMEM((groups * group_rows, matrix.shape[1]), jnp.float32),
            rows_shape(beside, matrix),
        ),
        in_specs=[VMEM] * (1 + len(weights)) + [ANY],
        out_specs=(VMEM, VMEM),
        scratch_shapes=[pltpu.SemaphoreType.DMA((beside[1],))],
        compiler_params=pltpu.CompilerParams(vmem_limit_bytes=2 * MIB),
        cost_estimate=pl.CostEstimate(flops=10**11, bytes_accessed=0, transcendentals=0),
        name="partial",
    )(rows, *weights, matrix)


def final_kernel(rows_ref, *refs, spans, late, batch_offsets, batch_count):
    early_refs, refs = refs[: len(spans)], refs[len(spans) :]
    (scores_ref, heat_ref, choice_ref, ids_ref, matrix_ref, keep_ref, send_ref) = refs[:7]
    late_ref, temp_ref, local_ids_ref, cand_ref, top_ref, total_ref, held_ref, sems = refs[7:]
    cols = scores_ref.shape[1]
    group_rows = rows_ref.shape[1]
    vocab_pos = lax.axis_index("vocab")
    batch_pos = lax.axis_index("batch")
    offset = (vocab_pos * batch_count + batch_pos) * cols
    slabs, _, width = late_ref.shape
    for n in range(slabs):
        slab_copy(late, n, matrix_ref, late_ref, sems).start()

    for s, j in enumerate(batch_offsets):
        rows = pl.ds(s * group_rows, group_rows)
        for row in range(group_rows):
            heat = heat_ref[choice_ref[(batch_pos ^ j) * group_rows + row]]
            temp_ref[pl.ds(s * group_rows + row, 1), :] = jnp.full((1, LANES), heat, jnp.float32)
        local_ids_ref[rows, :] = ids_ref[batch_pos ^ j] - offset
    cand_ref[...] = jnp.zeros_like(cand_ref)
    top_ref[...] = jnp.full_like(top_ref, -3e38)
    total_ref[...] = jnp.zeros_like(total_ref)

    parts = list(zip(early_refs, spans))

    def scores_of(n):
        at = n * width if isinstance(n, int) else pl.multiple_of(n * width, width)
        before = scores_ref[:, pl.ds(at, width)]
        return slab_scores(
            n, rows_ref, CHUNKS - 1, parts, late, matrix_ref, late_ref, sems, before
        )

    def count_in(n):
        scores = held_ref[n & 1]
        temp = temp_ref[...]
        local_ids = local_ids_ref[...]
        lane = local_ids & (LANES - 1)
        chunk_of = local_ids >> (LANES.bit_length() - 1)
        cand = cand_ref[...]
        chunks = []
        for c in range(width // LANES):
            scaled = scores[:, c * LANES : (c + 1) * LANES] / temp
            chunks.append(scaled)
            picked = jnp.take_along_axis(scaled, lane, axis=1, mode="promise_in_bounds")
            cand = jnp.where(chunk_of == n * (width // LANES) + c, picked, cand)
        cand_ref[...] = cand
        top = top_ref[...]
        new_top = functools.reduce(jnp.maximum, chunks, top)
        total = total_ref[...] * jnp.exp(top - new_top)
        for scaled in chunks:
            total = total + jnp.exp(scaled - new_top)
        top_ref[...] = new_top
        total_ref[...] = total

    held_ref[0] = scores_of(0)

    def step(n, carry):
        scores = scores_of(n)
        count_in(n - 1)
        held_ref[n & 1] = scores
        return carry

    lax.fori_loop(1, slabs, step, 0)
    count_in(slabs - 1)

    top = top_ref[...]
    row_top = jnp.max(top, axis=1, keepdims=True)
    row_total = jnp.sum(total_ref[...] * jnp.exp(top - row_top), axis=1, keepdims=True)
    row_log = jnp.broadcast_to(row_top + jnp.log(row_total), top.shape)
    for s, j in enumerate(batch_offsets):
        out_ref = send_ref if j & 1 else keep_ref
        out_ref[0, j // 2] = cand_ref[pl.ds(s * group_rows, group_rows), :]
        out_ref[1, j // 2] = row_log[s * group_rows : (s + 1) * group_rows]


def final(rows, early, spans, late, scores, heat, choice, ids, matrix, batch_offsets):
    batch_count, group_rows, _ = rows.shape
    slots, _ = scores.shape
    half = jax.ShapeDtypeStruct((2, batch_count // 2, group_rows, LANES), jnp.float32)
    rows_f32 = pltpu.VMEM((slots, LANES), jnp.float32)
    slabs = slabs_shape(late, matrix, 512)
    body = functools.partial(
        final_kernel, spans=spans, late=late, batch_offsets=batch_offsets, batch_count=batch_count
    )
    return pl.pallas_call(
        body,
        out_shape=(half, half),
        in_specs=[VMEM] * (len(early) + 2) + [SMEM, SMEM, VMEM, ANY],
        out_specs=(VMEM, VMEM),
        scratch_shapes=[
            slabs,
            rows_f32,
            pltpu.VMEM((slots, LANES), jnp.int32),
            rows_f32,
            rows_f32,
            rows_f32,
            pltpu.VMEM((2, slots, slabs.shape[2]), jnp.float32),
            pltpu.SemaphoreType.DMA((slabs.shape[0],)),
        ],
        compiler_params=pltpu.CompilerParams(
            vmem_limit_bytes=matrix.size // UNITS * late[1] * 2 + 3 * MIB
        ),
        name="final",
    )(rows, *early, scores, heat, choice, ids, matrix)


def joined(values):
    plane = lax.broadcasted_iota(jnp.int32, values[0].shape, 0)
    high = functools.reduce(jnp.maximum, values)
    total = sum(jnp.exp(value - high) for value in values)
    return jnp.where(plane == 0, sum(values), high + jnp.log(total))


def finish_kernel(keep_ref, *refs):
    *value_refs, log_ref, mass_ref, weights_ref, keep_rows_ref = refs
    group_rows, count = weights_ref.shape
    first = lax.axis_index("batch") * group_rows
    for row in range(group_rows):
        keep_rows_ref[pl.ds(row, 1), :] = jnp.full((1, count), keep_ref[first + row], jnp.int32)
    cand = sum(ref[0, 0] for ref in value_refs)
    logs = [ref[1, 0] for ref in value_refs]
    high = functools.reduce(jnp.maximum, logs)
    log_norm = high + jnp.log(sum(jnp.exp(value - high) for value in logs))
    lane = lax.broadcasted_iota(jnp.int32, (group_rows, count), 1)
    kept = lane < keep_rows_ref[...]
    top = jnp.max(jnp.where(kept, cand, jnp.float32(-3e38)), axis=1, keepdims=True)
    kept_exp = jnp.where(kept, jnp.exp(jnp.where(kept, cand - top, 0.0)), 0.0)
    kept_sum = jnp.sum(kept_exp, axis=1, keepdims=True)
    weights_ref[...] = kept_exp / kept_sum
    mass = jnp.broadcast_to(top + jnp.log(kept_sum), log_norm.shape) - log_norm
    own = lane == lax.broadcasted_iota(jnp.int32, lane.shape, 0)
    for ref, value in ((log_ref, log_norm), (mass_ref, mass)):
        row = jnp.sum(jnp.where(own, value, 0.0), axis=0, keepdims=True)
        ref[...] = row[:, :group_rows]


def finish(keep_count, values):
    group_rows, count = values[0].shape[2:]
    row = jax.ShapeDtypeStruct((1, group_rows), jnp.float32)
    log_norm, mass, weights = pl.pallas_call(
        finish_kernel,
        out_shape=(row, row, jax.ShapeDtypeStruct((group_rows, count), jnp.float32)),
        in_specs=[SMEM] + [VMEM] * len(values),
        out_specs=(VMEM,) * 3,
        scratch_shapes=[pltpu.VMEM((group_rows, count), jnp.int32)],
        compiler_params=pltpu.CompilerParams(vmem_limit_bytes=MIB),
        name="finish",
    )(keep_count, *values)
    return log_norm.reshape(-1), mass.reshape(-1), weights


def local(
    latent_state_rows,
    closing_rescale_coeffs,
    output_projection_matrix,
    config_heat_values,
    sequence_config_choice,
    ranked_choice_ids,
    keep_count,
):
    group_rows, _ = latent_state_rows.shape
    matrix = output_projection_matrix
    vocab_count = lax.axis_size("vocab")
    batch_count = lax.axis_size("batch")
    vocab_rounds = rounds_of(bits_of(vocab_count))
    vocab_bits = sum(vocab_rounds, [])
    batch_bits = bits_of(batch_count)[::-1]
    offsets = offsets_of(vocab_bits)
    batch_offsets = offsets_of(batch_bits)

    fetched, spans = [], []

    def fetch_next(after=None):
        span = (sum(spans[-1]) if spans else 0, EARLY_UNITS[len(spans)])
        spans.append(span)
        fetched.append(fetch(span, matrix, after))

    blocks = latent_state_rows[None]
    for n, bits in enumerate(vocab_rounds):
        others = []
        for offset in offsets_of(bits)[1:]:
            others.append(swap(blocks, "vocab", offset))
        if n < 2:
            fetch_next(blocks if n else None)
        blocks = jnp.concatenate([blocks, *others], axis=0)
    chunks = list(norm(blocks, closing_rescale_coeffs, offsets))
    for n, bit in enumerate(batch_bits):
        others = []
        for chunk in chunks:
            others.append(swap(chunk, "batch", bit))
        if n < 2:
            fetch_next(chunks[0])
        chunks = [jnp.concatenate(pair, axis=0) for pair in zip(chunks, others)]
    border = UNITS // CHUNKS
    mine = [n for n, span in enumerate(spans) if span[0] < border]
    beside = (sum(spans[-1]), BESIDE_UNITS)
    scores, extra = partial_scores(
        chunks[0], [fetched[n] for n in mine], [spans[n] for n in mine], matrix, beside
    )
    fetched.append(extra)
    spans.append(beside)
    late = (sum(beside), UNITS - sum(beside))
    rest = [n for n, span in enumerate(spans) if sum(span) > border]
    kept, sent = final(
        chunks[1],
        [fetched[n] for n in rest],
        [spans[n] for n in rest],
        late,
        scores,
        config_heat_values,
        sequence_config_choice,
        ranked_choice_ids.reshape(batch_count, group_rows, -1),
        matrix,
        batch_offsets,
    )
    kept = joined([kept, swap(sent, "batch", 1)])
    *vocab_rounds, near = vocab_rounds
    for bit in bits_of(batch_count)[1:]:
        half = [kept[:, 0::2], kept[:, 1::2]]
        values = [half[0], swap(half[1], "batch", bit)]
        if near:
            offset = near.pop()
            values += [swap(half[0], "vocab", offset), swap_both(half[1], offset, bit)]
        kept = joined(values)
    last = [kept]
    for bits in vocab_rounds[::-1] + [near]:
        if bits:
            kept = joined(last) if len(last) > 1 else kept
            last = [kept] + [swap(kept, "vocab", m) for m in offsets_of(bits)[:0:-1]]
    return finish(keep_count, last)


def solution(mesh):
    placed = (P("batch", "vocab"), P(), P(None, ("vocab", "batch")), P(), P(), P(), P())
    return jax.shard_map(
        local,
        mesh=mesh,
        in_specs=placed,
        out_specs=(P("batch"), P("batch"), P("batch", None)),
        check_vma=False,
    )
```

time: 240 us -> 61.1 us (0.25)
  blocking collectives: 115 us -> 0 us
  local copies, waits for them, and re-layouts: 65.7 us -> 0.09 us
  Pallas kernels: 0 us -> 31.3 us
  matrix products: 23.9 us -> 0 us
  starting transfers between devices: 0.04 us -> 18.1 us
  between operations: 14.1 us -> 0.91 us
  other arithmetic: 5.8 us -> 0.31 us
  waiting for transfers between devices: 14.8 us -> 10.2 us
    gather x1 -> x0, local copies, waits for them, and re-layouts: 65 us -> none  [local(): jnp.take_along_axis(divided_scores, jnp.clip(local_ids, 0, col_count - 1)...]
    psum x1 -> x0, blocking collectives: 41.3 us -> none  [local(): lax.psum(jnp.sum(jnp.exp(divided_scores - row_top[:, None]), axis=1), ('v...]
    pmax x1 -> x0, blocking collectives: 39.3 us -> none  [local(): row_top = lax.pmax(local_top, ('vocab', 'batch'))]
    all_gather x1 -> x0, blocking collectives: 34.8 us -> none  [local(): wide_rows = lax.all_gather(latent_state_rows, 'vocab', axis=1, tiled=True)]
    pallas_call x0 -> x8, Pallas kernels: none -> 31.3 us  [the longest x4 13.9 us: fetch(): pl.pallas_call(functools.partial(fetch_kernel, span=span), out_shape=rows...]
    dot_general x1 -> x0, matrix products: 23.9 us -> none  [local(): jnp.dot(rows_normed(lax.all_gather(wide_rows, 'batch', axis=0, tiled=True...]
    ppermute x0 -> x15, starting transfers between devices: none -> 18.1 us  [the longest x14 17.5 us: swap(): return lax.ppermute(value, axis, [(n, n ^ bit) for n in range(count)])]
    all_gather x1 -> x0, waiting for transfers between devices: 14.8 us -> none  [local(): lax.all_gather(wide_rows, 'batch', axis=0, tiled=True)]
  transfers between devices with their start and end apart: 1 -> 15, of which waited for: 1 -> 8; matrix products, arithmetic and copies ran while one was open for 1% -> 0% of each run, Pallas kernels for 0% -> 33%
where the time goes in v1:
time: 61.1 us; the launch traced here: 60.9 us
  Pallas kernels  31.3 us (51%)
  starting transfers between devices  18.1 us (30%)
  waiting for transfers between devices  10.2 us (17%)
  between operations  0.91 us (1%)
    ppermute x14, starting transfers between devices, swap(): return lax.ppermute(value, axis, [(n, n ^ bit) for n in range(count)])  17.5 us
    pallas_call x4, Pallas kernels, fetch(): pl.pallas_call(functools.partial(fetch_kernel, span=span), out_shape=rows...  13.9 us
    pallas_call x1, Pallas kernels, final(): pl.pallas_call(body, out_shape=(half, half), in_specs=[VMEM] * (len(early...  9.46 us
    ppermute x14, waiting for transfers between devices, swap(): return lax.ppermute(value, axis, [(n, n ^ bit) for n in range(count)])  7.94 us
    pallas_call x1, Pallas kernels, partial_scores(): pl.pallas_call(functools.partial(partial_kernel, spans=spans, beside=besi...  6.37 us
    ppermute x1, waiting for transfers between devices, swap_both(): return lax.ppermute(value, ('vocab', 'batch'), pairs)  2.31 us
    pallas_call x1, Pallas kernels, finish(): pl.pallas_call(finish_kernel, out_shape=(row, row, jax.ShapeDtypeStruct((...  1.35 us
  transfers between devices with their start and end apart: 15, of which 8 were waited for; matrix products, arithmetic and copies ran while one was open for 0% of the time, Pallas kernels for 33%

profile of v1, /device:TPU:0, one launch (start us, length us, event | category | flops | bytes accessed | tf_op | source)
XLA Modules:
  0.0 60.9 jit_solution(16033501258218884767)
XLA Ops:
  0.6 4.1 %collective-permute-start = (bf16[1,16,1024]{2,1,0:T(8,128)(2,1)}, bf16[1,16,1024]{2,1,0:T(8,128)(2,1)S(1)}, u32[]{:S(2)}, u32[]{:S(2)}) collective-permute-start(bf16[1,16,1024]{2,1,0:T(8,128)(2,1)} %bitcast.6), channel_id=1, source_target_pairs={{0,16},{4,20},{8,24},{12,28},{16,0},{20,4},{24,8},{28,12},{1,17},{... | collective-permute-start | bytes 98312 | tf_op jit(solution)/shard_map/ppermute | solution.py:32
  4.8 1.6 %collective-permute-start.1 = (bf16[1,16,1024]{2,1,0:T(8,128)(2,1)}, bf16[1,16,1024]{2,1,0:T(8,128)(2,1)S(1)}, u32[]{:S(2)}, u32[]{:S(2)}) collective-permute-start(bf16[1,16,1024]{2,1,0:T(8,128)(2,1)} %bitcast.7), channel_id=1, source_target_pairs={{0,8},{4,12},{8,0},{12,4},{16,24},{20,28},{24,16},{28,20},{1,9},{5... | collective-permute-start | bytes 98312 | tf_op jit(solution)/shard_map/ppermute | solution.py:32
  6.3 0.0 collective-permute-start.2
  6.3 4.7 %shard_map.94.refs_0_ = bf16[1536,4096]{1,0:T(8,128)(2,1)S(1)} custom-call(bf16[8192,4096]{1,0:T(8,128)(2,1)} %refs_5_.1), custom_call_target="tpu_custom_call" | custom-call | flops 60000002048 | bytes 12582912 | tf_op jit(solution)/shard_map/pallas_call | solution.py:87
  11.1 0.0 collective-permute-done
  11.1 0.0 collective-permute-done.1
  11.1 1.2 %collective-permute-done.2 = bf16[1,16,1024]{2,1,0:T(8,128)(2,1)S(1)} collective-permute-done((bf16[1,16,1024]{2,1,0:T(8,128)(2,1)}, bf16[1,16,1024]{2,1,0:T(8,128)(2,1)S(1)}, u32[]{:S(2)}, u32[]{:S(2)}) %collective-permute-start.2) | collective-permute-done | bytes 32800 | tf_op jit(solution)/shard_map/ppermute | solution.py:32
  12.3 0.0 copy-start.1
  12.3 1.6 %collective-permute-start.3 = (bf16[4,16,1024]{2,1,0:T(8,128)(2,1)S(1)}, bf16[4,16,1024]{2,1,0:T(8,128)(2,1)S(1)}, u32[]{:S(2)}, u32[]{:S(2)}) collective-permute-start(bf16[4,16,1024]{2,1,0:T(8,128)(2,1)S(1)} %pad_maximum_fusion.3.refs_0_), channel_id=1, source_target_pairs={{0,4},{4,0},{8,12},{12,8},{16,20},{20,16},{24,28},{28,24},{1,5},{5... | collective-permute-start | bytes 393224 | tf_op jit(solution)/shard_map/ppermute | solution.py:32
  13.9 3.5 %shard_map.95.refs_1_ = bf16[1024,4096]{1,0:T(8,128)(2,1)S(1)} custom-call(bf16[4,16,1024]{2,1,0:T(8,128)(2,1)S(1)} %pad_maximum_fusion.3.refs_0_, bf16[8192,4096]{1,0:T(8,128)(2,1)} %refs_5_.1), custom_call_target="tpu_custom_call" | custom-call | flops 40000000000 | bytes 8388608 | tf_op jit(solution)/shard_map/pallas_call | solution.py:87
  17.4 0.0 collective-permute-done.3
  17.5 0.0 copy-done.1
  17.5 0.2 norm.1
  17.7 1.6 %collective-permute-start.6 = (bf16[1,16,4096]{2,1,0:T(8,128)(2,1)S(1)}, bf16[1,16,4096]{2,1,0:T(8,128)(2,1)S(1)}, u32[]{:S(2)}, u32[]{:S(2)}) collective-permute-start(bf16[1,16,4096]{2,1,0:T(8,128)(2,1)S(1)} %get-tuple-element.13.refs_0_), channel_id=1, source_target_pairs={{0,2},{1,3},{2,0},{3,1},{4,6},{5,7},{6,4},{7,5},{8,10},{9,11},{10,... | collective-permute-start | bytes 393224 | tf_op jit(solution)/shard_map/ppermute | solution.py:32
  19.2 4.1 %shard_map.96.refs_2_ = bf16[1280,4096]{1,0:T(8,128)(2,1)S(1)} custom-call(bf16[1,16,4096]{2,1,0:T(8,128)(2,1)S(1)} %get-tuple-element.13.refs_0_, bf16[8192,4096]{1,0:T(8,128)(2,1)} %refs_5_.1), custom_call_target="tpu_custom_call" | custom-call | flops 49999998976 | bytes 10485760 | tf_op jit(solution)/shard_map/pallas_call | solution.py:87
  23.4 0.6 collective-permute-start.4
  24.0 0.0 collective-permute-done.6
  24.0 0.1 collective-permute-start.7
  24.0 1.6 %shard_map.97.refs_3_ = bf16[256,4096]{1,0:T(8,128)(2,1)S(1)} custom-call(bf16[2,16,4096]{2,1,0:T(8,128)(2,1)S(1)} %constant_dynamic-update-slice_fusion.5.refs_0_, bf16[8192,4096]{1,0:T(8,128)(2,1)} %refs_5_.1), custom_call_target="tpu_custom_call" | custom-call | flops 10000000000 | bytes 2097152 | tf_op jit(solution)/shard_map/pallas_call | solution.py:87
  25.7 2.7 %collective-permute-done.4 = bf16[1,16,4096]{2,1,0:T(8,128)(2,1)S(1)} collective-permute-done((bf16[1,16,4096]{2,1,0:T(8,128)(2,1)S(1)}, bf16[1,16,4096]{2,1,0:T(8,128)(2,1)S(1)}, u32[]{:S(2)}, u32[]{:S(2)}) %collective-permute-start.4) | collective-permute-done | bytes 131104 | tf_op jit(solution)/shard_map/ppermute | solution.py:32
  28.4 0.1 collective-permute-start.5
  28.5 0.0 collective-permute-done.7
  28.5 0.1 pad_maximum_fusion.1.rows_ref
  28.6 0.0 copy-start
  28.6 0.0 copy-start.2
  28.6 0.0 copy-start.3
  28.6 6.4 %partial.1 = (f32[64,4096]{1,0:T(8,128)S(1)}, bf16[1536,4096]{1,0:T(8,128)(2,1)S(1)}) custom-call(bf16[4,16,4096]{2,1,0:T(8,128)(2,1)S(1)} %pad_maximum_fusion.1.rows_ref, bf16[1536,4096]{1,0:T(8,128)(2,1)S(1)} %shard_map.94.refs_0_, bf16[1024,4096]{1,0:T(8,128)(2,1)S(1)} %shard_map.95.refs_1_, bf16[1280,4096]{1,0:T(8,128)(2,1)S(1)} %shard_map.96.refs_2_, ...), custom_call_target="tpu_custom_call" | custom-call | flops 99999997952 | tf_op jit(solution)/shard_map/partial/pallas_call | solution.py:206
  35.0 0.0 collective-permute-done.5
  35.0 0.1 pad_maximum_fusion.rows_ref
  35.1 0.0 copy-start.4
  35.1 9.5 %final.1 = (f32[2,2,16,128]{3,2,1,0:T(8,128)S(1)}, f32[2,2,16,128]{3,2,1,0:T(8,128)S(1)}) custom-call(bf16[4,16,4096]{2,1,0:T(8,128)(2,1)S(1)} %pad_maximum_fusion.rows_ref, bf16[1536,4096]{1,0:T(8,128)(2,1)S(1)} %get-tuple-element.14.refs_0_, f32[64,4096]{1,0:T(8,128)S(1)} %get-tuple-element.15.refs_1_, f32[16]{0:T(128)S(1)} %copy-done.2, s32[64]{0:T(128)S(1)} %copy-done.3, ...), custom_call_target="tpu_custom_call" | custom-call | tf_op jit(solution)/shard_map/final/pallas_call | solution.py:305
  44.6 0.6 collective-permute-start.8
  45.1 0.9 %collective-permute-done.8 = f32[2,2,16,128]{3,2,1,0:T(8,128)S(1)} collective-permute-done((f32[2,2,16,128]{3,2,1,0:T(8,128)S(1)}, f32[2,2,16,128]{3,2,1,0:T(8,128)S(1)}, u32[]{:S(2)}, u32[]{:S(2)}) %collective-permute-start.8) | collective-permute-done | bytes 32800 | tf_op jit(solution)/shard_map/ppermute | solution.py:32
  46.0 0.1 add_select_fusion
  46.1 1.5 %collective-permute-start.10 = (f32[2,1,16,128]{3,2,1,0:T(8,128)S(1)}, f32[2,1,16,128]{3,2,1,0:T(8,128)S(1)}, u32[]{:S(2)}, u32[]{:S(2)}) collective-permute-start(f32[2,1,16,128]{3,2,1,0:T(8,128)S(1)} %get-tuple-element.21), channel_id=1, source_target_pairs={{0,4},{4,0},{8,12},{12,8},{16,20},{20,16},{24,28},{28,24},{1,5},{5... | collective-permute-start | bytes 49160 | tf_op jit(solution)/shard_map/ppermute | solution.py:32
  47.5 0.6 collective-permute-start.11
  48.1 1.5 %collective-permute-start.9 = (f32[2,1,16,128]{3,2,1,0:T(8,128)S(1)}, f32[2,1,16,128]{3,2,1,0:T(8,128)S(1)}, u32[]{:S(2)}, u32[]{:S(2)}) collective-permute-start(f32[2,1,16,128]{3,2,1,0:T(8,128)S(1)} %get-tuple-element.22), channel_id=1, source_target_pairs={{0,2},{1,3},{2,0},{3,1},{4,6},{5,7},{6,4},{7,5},{8,10},{9,11},{10,... | collective-permute-start | bytes 49160 | tf_op jit(solution)/shard_map/ppermute | solution.py:32
  49.6 0.2 collective-permute-done.10
  49.8 2.3 %collective-permute-done.11 = f32[2,1,16,128]{3,2,1,0:T(8,128)S(1)} collective-permute-done((f32[2,1,16,128]{3,2,1,0:T(8,128)S(1)}, f32[2,1,16,128]{3,2,1,0:T(8,128)S(1)}, u32[]{:S(2)}, u32[]{:S(2)}) %collective-permute-start.11) | collective-permute-done | bytes 16416 | tf_op jit(solution)/shard_map/ppermute | solution.py:43
  52.2 0.0 collective-permute-done.9
  52.2 0.1 add_select_fusion.1.refs_0_
  52.2 2.7 %collective-permute-start.12 = (f32[2,1,16,128]{3,2,1,0:T(8,128)S(1)}, f32[2,1,16,128]{3,2,1,0:T(8,128)S(1)}, u32[]{:S(2)}, u32[]{:S(2)}) collective-permute-start(f32[2,1,16,128]{3,2,1,0:T(8,128)S(1)} %add_select_fusion.1.refs_0_), channel_id=1, source_target_pairs={{0,24},{4,28},{8,16},{12,20},{16,8},{20,12},{24,0},{28,4},{1,25},{... | collective-permute-start | bytes 49160 | tf_op jit(solution)/shard_map/ppermute | solution.py:32
  54.9 0.0 collective-permute-start.13
  54.9 1.7 %collective-permute-start.14 = (f32[2,1,16,128]{3,2,1,0:T(8,128)S(1)}, f32[2,1,16,128]{3,2,1,0:T(8,128)S(1)}, u32[]{:S(2)}, u32[]{:S(2)}) collective-permute-start(f32[2,1,16,128]{3,2,1,0:T(8,128)S(1)} %add_select_fusion.1.refs_0_), channel_id=1, source_target_pairs={{0,16},{4,20},{8,24},{12,28},{16,0},{20,4},{24,8},{28,12},{1,17},{... | collective-permute-start | bytes 49160 | tf_op jit(solution)/shard_map/ppermute | solution.py:32
  56.6 1.1 %collective-permute-done.12.refs_1_ = f32[2,1,16,128]{3,2,1,0:T(8,128)S(1)} collective-permute-done((f32[2,1,16,128]{3,2,1,0:T(8,128)S(1)}, f32[2,1,16,128]{3,2,1,0:T(8,128)S(1)}, u32[]{:S(2)}, u32[]{:S(2)}) %collective-permute-start.12) | collective-permute-done | bytes 16416 | tf_op jit(solution)/shard_map/ppermute | solution.py:32
  57.8 0.9 %collective-permute-done.13.refs_2_ = f32[2,1,16,128]{3,2,1,0:T(8,128)S(1)} collective-permute-done((f32[2,1,16,128]{3,2,1,0:T(8,128)S(1)}, f32[2,1,16,128]{3,2,1,0:T(8,128)S(1)}, u32[]{:S(2)}, u32[]{:S(2)}) %collective-permute-start.13) | collective-permute-done | bytes 16416 | tf_op jit(solution)/shard_map/ppermute | solution.py:32
  58.7 0.9 %collective-permute-done.14.refs_3_ = f32[2,1,16,128]{3,2,1,0:T(8,128)S(1)} collective-permute-done((f32[2,1,16,128]{3,2,1,0:T(8,128)S(1)}, f32[2,1,16,128]{3,2,1,0:T(8,128)S(1)}, u32[]{:S(2)}, u32[]{:S(2)}) %collective-permute-start.14) | collective-permute-done | bytes 16416 | tf_op jit(solution)/shard_map/ppermute | solution.py:32
  59.6 1.3 %finish.1 = (f32[1,16]{1,0:T(1,128)}, f32[1,16]{1,0:T(1,128)}, f32[16,128]{1,0:T(8,128)}) custom-call(s32[64]{0:T(128)S(1)} %copy-done.4, f32[2,1,16,128]{3,2,1,0:T(8,128)S(1)} %add_select_fusion.1.refs_0_, f32[2,1,16,128]{3,2,1,0:T(8,128)S(1)} %collective-permute-done.12.refs_1_, f32[2,1,16,128]{3,2,1,0:T(8,128)S(1)} %collective-permute-done.13.refs_2_, ...), custom_call_target="tpu_custom_call" | custom-call | tf_op jit(solution)/shard_map/finish/pallas_call | solution.py:360
  (17 shorter events, 0.1 us)
Async XLA Ops:
  0.6 10.4 %copy-start.5 = (bf16[16,1024]{1,0:T(8,128)(2,1)S(1)}, bf16[16,1024]{1,0:T(8,128)(2,1)}, u32[]{:S(2)}) copy-start(bf16[16,1024]{1,0:T(8,128)(2,1)} %param.7) | copy-start | bytes 98308
  0.6 10.5 %collective-permute-start = (bf16[1,16,1024]{2,1,0:T(8,128)(2,1)}, bf16[1,16,1024]{2,1,0:T(8,128)(2,1)S(1)}, u32[]{:S(2)}, u32[]{:S(2)}) collective-permute-start(bf16[1,16,1024]{2,1,0:T(8,128)(2,1)} %bitcast.6), channel_id=1, source_target_pairs={{0,16},{4,20},{8,24},{12,28},{16,0},{20,4},{24,8},{28,12},{1,17},{... | collective-permute-start | bytes 98312 | tf_op jit(solution)/shard_map/ppermute | solution.py:32
  4.8 6.3 %collective-permute-start.1 = (bf16[1,16,1024]{2,1,0:T(8,128)(2,1)}, bf16[1,16,1024]{2,1,0:T(8,128)(2,1)S(1)}, u32[]{:S(2)}, u32[]{:S(2)}) collective-permute-start(bf16[1,16,1024]{2,1,0:T(8,128)(2,1)} %bitcast.7), channel_id=1, source_target_pairs={{0,8},{4,12},{8,0},{12,4},{16,24},{20,28},{24,16},{28,20},{1,9},{5... | collective-permute-start | bytes 98312 | tf_op jit(solution)/shard_map/ppermute | solution.py:32
  6.3 5.9 %collective-permute-start.2 = (bf16[1,16,1024]{2,1,0:T(8,128)(2,1)}, bf16[1,16,1024]{2,1,0:T(8,128)(2,1)S(1)}, u32[]{:S(2)}, u32[]{:S(2)}) collective-permute-start(bf16[1,16,1024]{2,1,0:T(8,128)(2,1)} %bitcast.8), channel_id=1, source_target_pairs={{0,24},{4,28},{8,16},{12,20},{16,8},{20,12},{24,0},{28,4},{1,25},{... | collective-permute-start | bytes 98312 | tf_op jit(solution)/shard_map/ppermute | solution.py:32
  12.3 5.2 %copy-start.1 = (bf16[8192]{0:T(1024)(128)(2,1)S(1)}, bf16[8192]{0:T(1024)(128)(2,1)}, u32[]{:S(2)}) copy-start(bf16[8192]{0:T(1024)(128)(2,1)} %gain_ref.1) | copy-start | bytes 49156
  12.3 5.1 %collective-permute-start.3 = (bf16[4,16,1024]{2,1,0:T(8,128)(2,1)S(1)}, bf16[4,16,1024]{2,1,0:T(8,128)(2,1)S(1)}, u32[]{:S(2)}, u32[]{:S(2)}) collective-permute-start(bf16[4,16,1024]{2,1,0:T(8,128)(2,1)S(1)} %pad_maximum_fusion.3.refs_0_), channel_id=1, source_target_pairs={{0,4},{4,0},{8,12},{12,8},{16,20},{20,16},{24,28},{28,24},{1,5},{5... | collective-permute-start | bytes 393224 | tf_op jit(solution)/shard_map/ppermute | solution.py:32
  17.7 6.3 %collective-permute-start.6 = (bf16[1,16,4096]{2,1,0:T(8,128)(2,1)S(1)}, bf16[1,16,4096]{2,1,0:T(8,128)(2,1)S(1)}, u32[]{:S(2)}, u32[]{:S(2)}) collective-permute-start(bf16[1,16,4096]{2,1,0:T(8,128)(2,1)S(1)} %get-tuple-element.13.refs_0_), channel_id=1, source_target_pairs={{0,2},{1,3},{2,0},{3,1},{4,6},{5,7},{6,4},{7,5},{8,10},{9,11},{10,... | collective-permute-start | bytes 393224 | tf_op jit(solution)/shard_map/ppermute | solution.py:32
  23.4 5.0 %collective-permute-start.4 = (bf16[1,16,4096]{2,1,0:T(8,128)(2,1)S(1)}, bf16[1,16,4096]{2,1,0:T(8,128)(2,1)S(1)}, u32[]{:S(2)}, u32[]{:S(2)}) collective-permute-start(bf16[1,16,4096]{2,1,0:T(8,128)(2,1)S(1)} %get-tuple-element.12), channel_id=1, source_target_pairs={{0,2},{1,3},{2,0},{3,1},{4,6},{5,7},{6,4},{7,5},{8,10},{9,11},{10,... | collective-permute-start | bytes 393224 | tf_op jit(solution)/shard_map/ppermute | solution.py:32
  24.0 4.5 %collective-permute-start.7 = (bf16[2,16,4096]{2,1,0:T(8,128)(2,1)S(1)}, bf16[2,16,4096]{2,1,0:T(8,128)(2,1)S(1)}, u32[]{:S(2)}, u32[]{:S(2)}) collective-permute-start(bf16[2,16,4096]{2,1,0:T(8,128)(2,1)S(1)} %constant_dynamic-update-slice_fusion.5.refs_0_), channel_id=1, source_target_pairs={{0,1},{1,0},{2,3},{3,2},{4,5},{5,4},{6,7},{7,6},{8,9},{9,8},{10,11... | collective-permute-start | bytes 786440 | tf_op jit(solution)/shard_map/ppermute | solution.py:32
  28.4 6.6 %collective-permute-start.5 = (bf16[2,16,4096]{2,1,0:T(8,128)(2,1)S(1)}, bf16[2,16,4096]{2,1,0:T(8,128)(2,1)S(1)}, u32[]{:S(2)}, u32[]{:S(2)}) collective-permute-start(bf16[2,16,4096]{2,1,0:T(8,128)(2,1)S(1)} %pad_maximum_fusion.2), channel_id=1, source_target_pairs={{0,1},{1,0},{2,3},{3,2},{4,5},{5,4},{6,7},{7,6},{8,9},{9,8},{10,11... | collective-permute-start | bytes 786440 | tf_op jit(solution)/shard_map/ppermute | solution.py:32
  28.6 6.5 %copy-start = (s32[64,128]{1,0:T(8,128)S(1)}, s32[64,128]{1,0:T(8,128)}, u32[]{:S(2)}) copy-start(s32[64,128]{1,0:T(8,128)} %param.12) | copy-start | bytes 98308
  28.6 6.5 %copy-start.2 = (f32[16]{0:T(128)S(1)}, f32[16]{0:T(128)}, u32[]{:S(2)}) copy-start(f32[16]{0:T(128)} %refs_2_.1) | copy-start | bytes 196
  28.6 6.5 %copy-start.3 = (s32[64]{0:T(128)S(1)}, s32[64]{0:T(128)}, u32[]{:S(2)}) copy-start(s32[64]{0:T(128)} %refs_3_.1) | copy-start | bytes 772
  35.1 24.5 %copy-start.4 = (s32[64]{0:T(128)S(1)}, s32[64]{0:T(128)}, u32[]{:S(2)}) copy-start(s32[64]{0:T(128)} %keep_ref.1) | copy-start | bytes 772
  44.6 1.4 %collective-permute-start.8 = (f32[2,2,16,128]{3,2,1,0:T(8,128)S(1)}, f32[2,2,16,128]{3,2,1,0:T(8,128)S(1)}, u32[]{:S(2)}, u32[]{:S(2)}) collective-permute-start(f32[2,2,16,128]{3,2,1,0:T(8,128)S(1)} %get-tuple-element.17), channel_id=1, source_target_pairs={{0,1},{1,0},{2,3},{3,2},{4,5},{5,4},{6,7},{7,6},{8,9},{9,8},{10,11... | collective-permute-start | bytes 98312 | tf_op jit(solution)/shard_map/ppermute | solution.py:32
  46.1 3.8 %collective-permute-start.10 = (f32[2,1,16,128]{3,2,1,0:T(8,128)S(1)}, f32[2,1,16,128]{3,2,1,0:T(8,128)S(1)}, u32[]{:S(2)}, u32[]{:S(2)}) collective-permute-start(f32[2,1,16,128]{3,2,1,0:T(8,128)S(1)} %get-tuple-element.21), channel_id=1, source_target_pairs={{0,4},{4,0},{8,12},{12,8},{16,20},{20,16},{24,28},{28,24},{1,5},{5... | collective-permute-start | bytes 49160 | tf_op jit(solution)/shard_map/ppermute | solution.py:32
  47.5 4.6 %collective-permute-start.11 = (f32[2,1,16,128]{3,2,1,0:T(8,128)S(1)}, f32[2,1,16,128]{3,2,1,0:T(8,128)S(1)}, u32[]{:S(2)}, u32[]{:S(2)}) collective-permute-start(f32[2,1,16,128]{3,2,1,0:T(8,128)S(1)} %get-tuple-element.22), channel_id=1, source_target_pairs={{0,6},{1,7},{2,4},{3,5},{4,2},{5,3},{6,0},{7,1},{8,14},{9,15},{10,... | collective-permute-start | bytes 49160 | tf_op jit(solution)/shard_map/ppermute | solution.py:43
  48.1 4.0 %collective-permute-start.9 = (f32[2,1,16,128]{3,2,1,0:T(8,128)S(1)}, f32[2,1,16,128]{3,2,1,0:T(8,128)S(1)}, u32[]{:S(2)}, u32[]{:S(2)}) collective-permute-start(f32[2,1,16,128]{3,2,1,0:T(8,128)S(1)} %get-tuple-element.22), channel_id=1, source_target_pairs={{0,2},{1,3},{2,0},{3,1},{4,6},{5,7},{6,4},{7,5},{8,10},{9,11},{10,... | collective-permute-start | bytes 49160 | tf_op jit(solution)/shard_map/ppermute | solution.py:32
  52.2 5.6 %collective-permute-start.12 = (f32[2,1,16,128]{3,2,1,0:T(8,128)S(1)}, f32[2,1,16,128]{3,2,1,0:T(8,128)S(1)}, u32[]{:S(2)}, u32[]{:S(2)}) collective-permute-start(f32[2,1,16,128]{3,2,1,0:T(8,128)S(1)} %add_select_fusion.1.refs_0_), channel_id=1, source_target_pairs={{0,24},{4,28},{8,16},{12,20},{16,8},{20,12},{24,0},{28,4},{1,25},{... | collective-permute-start | bytes 49160 | tf_op jit(solution)/shard_map/ppermute | solution.py:32
  54.9 3.7 %collective-permute-start.13 = (f32[2,1,16,128]{3,2,1,0:T(8,128)S(1)}, f32[2,1,16,128]{3,2,1,0:T(8,128)S(1)}, u32[]{:S(2)}, u32[]{:S(2)}) collective-permute-start(f32[2,1,16,128]{3,2,1,0:T(8,128)S(1)} %add_select_fusion.1.refs_0_), channel_id=1, source_target_pairs={{0,8},{4,12},{8,0},{12,4},{16,24},{20,28},{24,16},{28,20},{1,9},{5... | collective-permute-start | bytes 49160 | tf_op jit(solution)/shard_map/ppermute | solution.py:32
  54.9 4.6 %collective-permute-start.14 = (f32[2,1,16,128]{3,2,1,0:T(8,128)S(1)}, f32[2,1,16,128]{3,2,1,0:T(8,128)S(1)}, u32[]{:S(2)}, u32[]{:S(2)}) collective-permute-start(f32[2,1,16,128]{3,2,1,0:T(8,128)S(1)} %add_select_fusion.1.refs_0_), channel_id=1, source_target_pairs={{0,16},{4,20},{8,24},{12,28},{16,0},{20,4},{24,8},{28,12},{1,17},{... | collective-permute-start | bytes 49160 | tf_op jit(solution)/shard_map/ppermute | solution.py:32

commit v2 on v1

--- a/solution.py
+++ b/solution.py
@@ -13,9 +13,9 @@
 UNITS = 32
 CHUNKS = 2
 EARLY_UNITS = (6, 4, 5, 1)
-BESIDE_UNITS = 6
+BESIDE_UNITS = 7
 MIB = 1 << 20
-SLAB = 1024
+SLAB = 2048
 
 
 VMEM = pl.BlockSpec(memory_space=pltpu.VMEM)
@@ -95,6 +95,50 @@
             flops=span[1] * 10**10, bytes_accessed=matrix.size * 2 // UNITS * span[1], transcendentals=0
         ),
     )(*operands)
+
+
+def table_fetch_kernel(
+    after_ref, heat_ref, choice_ref, keep_ref, ids_ref, matrix_ref, *refs, span, order
+):
+    out_ref, temp_ref, local_ids_ref, keep_rows_ref, sems = refs
+    copies = unit_copies(span, matrix_ref, out_ref, sems)
+    for copy in copies:
+        copy.start()
+    group_rows = keep_rows_ref.shape[0]
+    batch_pos = lax.axis_index("batch")
+    place = lax.axis_index("vocab") * lax.axis_size("batch") + batch_pos
+    for s, j in enumerate(order):
+        first = (batch_pos ^ j) * group_rows
+        rows = pl.ds(s * group_rows, group_rows)
+        local_ids_ref[rows, :] = ids_ref[batch_pos ^ j] - place * matrix_ref.shape[1]
+        for row in range(group_rows):
+            heat = heat_ref[choice_ref[first + row]]
+            temp_ref[pl.ds(s * group_rows + row, 1), :] = jnp.full((1, LANES), heat, jnp.float32)
+    for row in range(group_rows):
+        keep = keep_ref[batch_pos * group_rows + row]
+        keep_rows_ref[pl.ds(row, 1), :] = jnp.full((1, LANES), keep, jnp.int32)
+    for copy in copies:
+        copy.wait()
+
+
+def table_fetch(span, after, heat, choice, keep, ids, matrix, order):
+    groups, group_rows, _ = ids.shape
+    slots = groups * group_rows
+    return pl.pallas_call(
+        functools.partial(table_fetch_kernel, span=span, order=order),
+        out_shape=(
+            rows_shape(span, matrix),
+            jax.ShapeDtypeStruct((slots, LANES), jnp.float32),
+            jax.ShapeDtypeStruct((slots, LANES), jnp.int32),
+            jax.ShapeDtypeStruct((group_rows, LANES), jnp.int32),
+        ),
+        in_specs=[ANY, SMEM, SMEM, SMEM, VMEM, ANY],
+        out_specs=(VMEM,) * 4,
+        scratch_shapes=[pltpu.SemaphoreType.DMA((span[1],))],
+        compiler_params=pltpu.CompilerParams(vmem_limit_bytes=MIB),
+        cost_estimate=pl.CostEstimate(flops=10**11, bytes_accessed=0, transcendentals=0),
+        name="tables",
+    )(after, heat, choice, keep, ids, matrix)
 
 
 def norm_kernel(pieces_ref, gain_ref, *out_refs, offsets):
@@ -218,25 +262,17 @@
     )(rows, *weights, matrix)
 
 
-def final_kernel(rows_ref, *refs, spans, late, batch_offsets, batch_count):
+def final_kernel(
+    rows_ref, *refs, spans, late, batch_offsets
+):
     early_refs, refs = refs[: len(spans)], refs[len(spans) :]
-    (scores_ref, heat_ref, choice_ref, ids_ref, matrix_ref, keep_ref, send_ref) = refs[:7]
-    late_ref, temp_ref, local_ids_ref, cand_ref, top_ref, total_ref, held_ref, sems = refs[7:]
-    cols = scores_ref.shape[1]
+    (scores_ref, temp_ref, local_ids_ref, matrix_ref, keep_ref, send_ref) = refs[:6]
+    late_ref, cand_ref, top_ref, total_ref, held_ref, sems = refs[6:]
     group_rows = rows_ref.shape[1]
-    vocab_pos = lax.axis_index("vocab")
-    batch_pos = lax.axis_index("batch")
-    offset = (vocab_pos * batch_count + batch_pos) * cols
     slabs, _, width = late_ref.shape
     for n in range(slabs):
         slab_copy(late, n, matrix_ref, late_ref, sems).start()
 
-    for s, j in enumerate(batch_offsets):
-        rows = pl.ds(s * group_rows, group_rows)
-        for row in range(group_rows):
-            heat = heat_ref[choice_ref[(batch_pos ^ j) * group_rows + row]]
-            temp_ref[pl.ds(s * group_rows + row, 1), :] = jnp.full((1, LANES), heat, jnp.float32)
-        local_ids_ref[rows, :] = ids_ref[batch_pos ^ j] - offset
     cand_ref[...] = jnp.zeros_like(cand_ref)
     top_ref[...] = jnp.full_like(top_ref, -3e38)
     total_ref[...] = jnp.zeros_like(total_ref)
@@ -293,24 +329,25 @@
         out_ref[1, j // 2] = row_log[s * group_rows : (s + 1) * group_rows]
 
 
-def final(rows, early, spans, late, scores, heat, choice, ids, matrix, batch_offsets):
+def final(rows, early, spans, late, scores, temp, local_ids, matrix, batch_offsets):
     batch_count, group_rows, _ = rows.shape
     slots, _ = scores.shape
     half = jax.ShapeDtypeStruct((2, batch_count // 2, group_rows, LANES), jnp.float32)
     rows_f32 = pltpu.VMEM((slots, LANES), jnp.float32)
     slabs = slabs_shape(late, matrix, 512)
     body = functools.partial(
-        final_kernel, spans=spans, late=late, batch_offsets=batch_offsets, batch_count=batch_count
+        final_kernel,
+        spans=spans,
+        late=late,
+        batch_offsets=batch_offsets,
     )
     return pl.pallas_call(
         body,
         out_shape=(half, half),
-        in_specs=[VMEM] * (len(early) + 2) + [SMEM, SMEM, VMEM, ANY],
+        in_specs=[VMEM] * (len(early) + 4) + [ANY],
         out_specs=(VMEM, VMEM),
         scratch_shapes=[
             slabs,
-            rows_f32,
-            pltpu.VMEM((slots, LANES), jnp.int32),
             rows_f32,
             rows_f32,
             rows_f32,
@@ -321,7 +358,7 @@
             vmem_limit_bytes=matrix.size // UNITS * late[1] * 2 + 3 * MIB
         ),
         name="final",
-    )(rows, *early, scores, heat, choice, ids, matrix)
+    )(rows, *early, scores, temp, local_ids, matrix)
 
 
 def joined(values):
@@ -331,12 +368,9 @@
     return jnp.where(plane == 0, sum(values), high + jnp.log(total))
 
 
-def finish_kernel(keep_ref, *refs):
-    *value_refs, log_ref, mass_ref, weights_ref, keep_rows_ref = refs
+def finish_kernel(keep_rows_ref, *refs):
+    *value_refs, log_ref, mass_ref, weights_ref = refs
     group_rows, count = weights_ref.shape
-    first = lax.axis_index("batch") * group_rows
-    for row in range(group_rows):
-        keep_rows_ref[pl.ds(row, 1), :] = jnp.full((1, count), keep_ref[first + row], jnp.int32)
     cand = sum(ref[0, 0] for ref in value_refs)
     logs = [ref[1, 0] for ref in value_refs]
     high = functools.reduce(jnp.maximum, logs)
@@ -354,18 +388,17 @@
         ref[...] = row[:, :group_rows]
 
 
-def finish(keep_count, values):
+def finish(keep_rows, values):
     group_rows, count = values[0].shape[2:]
     row = jax.ShapeDtypeStruct((1, group_rows), jnp.float32)
     log_norm, mass, weights = pl.pallas_call(
         finish_kernel,
         out_shape=(row, row, jax.ShapeDtypeStruct((group_rows, count), jnp.float32)),
-        in_specs=[SMEM] + [VMEM] * len(values),
+        in_specs=[VMEM] * (1 + len(values)),
         out_specs=(VMEM,) * 3,
-        scratch_shapes=[pltpu.VMEM((group_rows, count), jnp.int32)],
         compiler_params=pltpu.CompilerParams(vmem_limit_bytes=MIB),
         name="finish",
-    )(keep_count, *values)
+    )(keep_rows, *values)
     return log_norm.reshape(-1), mass.reshape(-1), weights
 
 
@@ -408,7 +441,20 @@
         others = []
         for chunk in chunks:
             others.append(swap(chunk, "batch", bit))
-        if n < 2:
+        if n == 0:
+            spans.append((sum(spans[-1]), EARLY_UNITS[2]))
+            weights, temp, local_ids, keep_rows = table_fetch(
+                spans[-1],
+                chunks[0],
+                config_heat_values,
+                sequence_config_choice,
+                keep_count,
+                ranked_choice_ids.reshape(batch_count, group_rows, -1),
+                matrix,
+                batch_offsets,
+            )
+            fetched.append(weights)
+        elif n == 1:
             fetch_next(chunks[0])
         chunks = [jnp.concatenate(pair, axis=0) for pair in zip(chunks, others)]
     border = UNITS // CHUNKS
@@ -427,9 +473,8 @@
         [spans[n] for n in rest],
         late,
         scores,
-        config_heat_values,
-        sequence_config_choice,
-        ranked_choice_ids.reshape(batch_count, group_rows, -1),
+        temp,
+        local_ids,
         matrix,
         batch_offsets,
     )
@@ -447,7 +492,7 @@
         if bits:
             kept = joined(last) if len(last) > 1 else kept
             last = [kept] + [swap(kept, "vocab", m) for m in offsets_of(bits)[:0:-1]]
-    return finish(keep_count, last)
+    return finish(keep_rows, last)
 
 
 def solution(mesh):

time: 61.1 us -> 58.3 us (0.954)
  waiting for transfers between devices: 10.2 us -> 8.49 us
  Pallas kernels: 31.3 us -> 30.3 us
    pallas_call x0 -> x1, Pallas kernels: none -> 4.66 us  [table_fetch(): pl.pallas_call(functools.partial(table_fetch_kernel, span=span, order=ord...]
    pallas_call x4 -> x3, Pallas kernels: 13.9 us -> 9.81 us  [fetch(): pl.pallas_call(functools.partial(fetch_kernel, span=span), out_shape=rows...]
    ppermute x14, waiting for transfers between devices: 7.94 us -> 6.14 us  [swap(): return lax.ppermute(value, axis, [(n, n ^ bit) for n in range(count)])]
    ppermute x14, starting transfers between devices: 17.5 us -> 16.5 us  [swap(): return lax.ppermute(value, axis, [(n, n ^ bit) for n in range(count)])]
    ppermute x1, starting transfers between devices: 0.59 us -> 1.55 us  [swap_both(): return lax.ppermute(value, ('vocab', 'batch'), pairs)]
    pallas_call x1, Pallas kernels: 9.46 us -> 8.77 us  [final(): pl.pallas_call(body, out_shape=(half, half), in_specs=[VMEM] * (len(early...]
  transfers between devices with their start and end apart: 15 -> 15, of which waited for: 8 -> 8; matrix products, arithmetic and copies ran while one was open for 0% -> 0% of each run, Pallas kernels for 33% -> 35%
where the time goes in v2:
time: 58.3 us; the launch traced here: 58.2 us
  Pallas kernels  30.3 us (52%)
  starting transfers between devices  18 us (31%)
  waiting for transfers between devices  8.49 us (15%)
  between operations  0.9 us (2%)
    ppermute x14, starting transfers between devices, swap(): return lax.ppermute(value, axis, [(n, n ^ bit) for n in range(count)])  16.5 us
    pallas_call x3, Pallas kernels, fetch(): pl.pallas_call(functools.partial(fetch_kernel, span=span), out_shape=rows...  9.81 us
    pallas_call x1, Pallas kernels, final(): pl.pallas_call(body, out_shape=(half, half), in_specs=[VMEM] * (len(early...  8.77 us
    ppermute x14, waiting for transfers between devices, swap(): return lax.ppermute(value, axis, [(n, n ^ bit) for n in range(count)])  6.14 us
    pallas_call x1, Pallas kernels, partial_scores(): pl.pallas_call(functools.partial(partial_kernel, spans=spans, beside=besi...  6.12 us
    pallas_call x1, Pallas kernels, table_fetch(): pl.pallas_call(functools.partial(table_fetch_kernel, span=span, order=ord...  4.66 us
    ppermute x1, waiting for transfers between devices, swap_both(): return lax.ppermute(value, ('vocab', 'batch'), pairs)  2.34 us
    ppermute x1, starting transfers between devices, swap_both(): return lax.ppermute(value, ('vocab', 'batch'), pairs)  1.55 us
  transfers between devices with their start and end apart: 15, of which 8 were waited for; matrix products, arithmetic and copies ran while one was open for 0% of the time, Pallas kernels for 35%

profile of v2, /device:TPU:0, one launch (start us, length us, event | category | flops | bytes accessed | tf_op | source)
XLA Modules:
  0.0 58.2 jit_solution(475352043480492897)
XLA Ops:
  0.6 4.1 %collective-permute-start = (bf16[1,16,1024]{2,1,0:T(8,128)(2,1)}, bf16[1,16,1024]{2,1,0:T(8,128)(2,1)S(1)}, u32[]{:S(2)}, u32[]{:S(2)}) collective-permute-start(bf16[1,16,1024]{2,1,0:T(8,128)(2,1)} %bitcast.6), channel_id=1, source_target_pairs={{0,16},{4,20},{8,24},{12,28},{16,0},{20,4},{24,8},{28,12},{1,17},{... | collective-permute-start | bytes 98312 | tf_op jit(solution)/shard_map/ppermute | solution.py:32
  4.8 1.6 %collective-permute-start.1 = (bf16[1,16,1024]{2,1,0:T(8,128)(2,1)}, bf16[1,16,1024]{2,1,0:T(8,128)(2,1)S(1)}, u32[]{:S(2)}, u32[]{:S(2)}) collective-permute-start(bf16[1,16,1024]{2,1,0:T(8,128)(2,1)} %bitcast.7), channel_id=1, source_target_pairs={{0,8},{4,12},{8,0},{12,4},{16,24},{20,28},{24,16},{28,20},{1,9},{5... | collective-permute-start | bytes 98312 | tf_op jit(solution)/shard_map/ppermute | solution.py:32
  6.3 0.0 collective-permute-start.2
  6.3 4.7 %shard_map.94.refs_0_ = bf16[1536,4096]{1,0:T(8,128)(2,1)S(1)} custom-call(bf16[8192,4096]{1,0:T(8,128)(2,1)} %refs_4_.3), custom_call_target="tpu_custom_call" | custom-call | flops 60000002048 | bytes 12582912 | tf_op jit(solution)/shard_map/pallas_call | solution.py:87
  11.1 0.0 collective-permute-done
  11.1 0.0 collective-permute-done.1
  11.1 1.2 %collective-permute-done.2 = bf16[1,16,1024]{2,1,0:T(8,128)(2,1)S(1)} collective-permute-done((bf16[1,16,1024]{2,1,0:T(8,128)(2,1)}, bf16[1,16,1024]{2,1,0:T(8,128)(2,1)S(1)}, u32[]{:S(2)}, u32[]{:S(2)}) %collective-permute-start.2) | collective-permute-done | bytes 32800 | tf_op jit(solution)/shard_map/ppermute | solution.py:32
  12.3 0.0 copy-start
  12.3 0.0 copy-start.1
  12.3 0.0 copy-start.2
  12.3 0.0 copy-start.3
  12.3 0.0 copy-start.4
  12.4 1.6 %collective-permute-start.3 = (bf16[4,16,1024]{2,1,0:T(8,128)(2,1)S(1)}, bf16[4,16,1024]{2,1,0:T(8,128)(2,1)S(1)}, u32[]{:S(2)}, u32[]{:S(2)}) collective-permute-start(bf16[4,16,1024]{2,1,0:T(8,128)(2,1)S(1)} %pad_maximum_fusion.3.refs_0_), channel_id=1, source_target_pairs={{0,4},{4,0},{8,12},{12,8},{16,20},{20,16},{24,28},{28,24},{1,5},{5... | collective-permute-start | bytes 393224 | tf_op jit(solution)/shard_map/ppermute | solution.py:32
  13.9 3.5 %shard_map.95.refs_1_ = bf16[1024,4096]{1,0:T(8,128)(2,1)S(1)} custom-call(bf16[4,16,1024]{2,1,0:T(8,128)(2,1)S(1)} %pad_maximum_fusion.3.refs_0_, bf16[8192,4096]{1,0:T(8,128)(2,1)} %refs_4_.3), custom_call_target="tpu_custom_call" | custom-call | flops 40000000000 | bytes 8388608 | tf_op jit(solution)/shard_map/pallas_call | solution.py:87
  17.5 0.0 collective-permute-done.3
  17.5 0.0 copy-done
  17.5 0.2 norm.1
  17.7 1.6 %collective-permute-start.6 = (bf16[1,16,4096]{2,1,0:T(8,128)(2,1)S(1)}, bf16[1,16,4096]{2,1,0:T(8,128)(2,1)S(1)}, u32[]{:S(2)}, u32[]{:S(2)}) collective-permute-start(bf16[1,16,4096]{2,1,0:T(8,128)(2,1)S(1)} %get-tuple-element.16.after_ref), channel_id=1, source_target_pairs={{0,2},{1,3},{2,0},{3,1},{4,6},{5,7},{6,4},{7,5},{8,10},{9,11},{10,... | collective-permute-start | bytes 393224 | tf_op jit(solution)/shard_map/ppermute | solution.py:32
  19.3 0.5 collective-permute-start.4
  19.8 4.7 %tables.1 = (bf16[1280,4096]{1,0:T(8,128)(2,1)S(1)}, f32[64,128]{1,0:T(8,128)S(1)}, s32[64,128]{1,0:T(8,128)S(1)}, s32[16,128]{1,0:T(8,128)S(1)}) custom-call(bf16[1,16,4096]{2,1,0:T(8,128)(2,1)S(1)} %get-tuple-element.16.after_ref, f32[16]{0:T(128)S(1)} %copy-done.2, s32[64]{0:T(128)S(1)} %copy-done.3, s32[64]{0:T(128)S(1)} %copy-done.4, ...), custom_call_target="tpu_custom_call" | custom-call | flops 99999997952 | tf_op jit(solution)/shard_map/tables/pallas_call | solution.py:127
  24.5 0.0 collective-permute-done.6
  24.5 0.1 collective-permute-start.7
  24.6 1.6 %shard_map.96.refs_3_ = bf16[256,4096]{1,0:T(8,128)(2,1)S(1)} custom-call(bf16[2,16,4096]{2,1,0:T(8,128)(2,1)S(1)} %constant_dynamic-update-slice_fusion.5.refs_0_, bf16[8192,4096]{1,0:T(8,128)(2,1)} %refs_4_.3), custom_call_target="tpu_custom_call" | custom-call | flops 10000000000 | bytes 2097152 | tf_op jit(solution)/shard_map/pallas_call | solution.py:87
  26.2 0.0 collective-permute-done.4
  26.3 0.6 collective-permute-start.5
  26.8 0.0 collective-permute-done.7
  26.8 0.1 pad_maximum_fusion.1.rows_ref
  26.9 6.1 %partial.1 = (f32[64,4096]{1,0:T(8,128)S(1)}, bf16[1792,4096]{1,0:T(8,128)(2,1)S(1)}) custom-call(bf16[4,16,4096]{2,1,0:T(8,128)(2,1)S(1)} %pad_maximum_fusion.1.rows_ref, bf16[1536,4096]{1,0:T(8,128)(2,1)S(1)} %shard_map.94.refs_0_, bf16[1024,4096]{1,0:T(8,128)(2,1)S(1)} %shard_map.95.refs_1_, bf16[1280,4096]{1,0:T(8,128)(2,1)S(1)} %get-tuple-element.19.refs_2_, ...), custom_call_target="tpu_custom_call" | custom-call | flops 99999997952 | tf_op jit(solution)/shard_map/partial/pallas_call | solution.py:250
  33.0 0.0 collective-permute-done.5
  33.0 0.1 pad_maximum_fusion.rows_ref
  33.1 8.8 %final.1 = (f32[2,2,16,128]{3,2,1,0:T(8,128)S(1)}, f32[2,2,16,128]{3,2,1,0:T(8,128)S(1)}) custom-call(bf16[4,16,4096]{2,1,0:T(8,128)(2,1)S(1)} %pad_maximum_fusion.rows_ref, bf16[1792,4096]{1,0:T(8,128)(2,1)S(1)} %get-tuple-element.20.refs_0_, f32[64,4096]{1,0:T(8,128)S(1)} %get-tuple-element.21.refs_1_, f32[64,128]{1,0:T(8,128)S(1)} %get-tuple-element.22.refs_2_, ...), custom_call_target="tpu_custom_call" | custom-call | tf_op jit(solution)/shard_map/final/pallas_call | solution.py:344
  41.9 0.1 collective-permute-start.8
  42.0 1.2 %collective-permute-done.8 = f32[2,2,16,128]{3,2,1,0:T(8,128)S(1)} collective-permute-done((f32[2,2,16,128]{3,2,1,0:T(8,128)S(1)}, f32[2,2,16,128]{3,2,1,0:T(8,128)S(1)}, u32[]{:S(2)}, u32[]{:S(2)}) %collective-permute-start.8) | collective-permute-done | bytes 32800 | tf_op jit(solution)/shard_map/ppermute | solution.py:32
  43.1 0.1 add_select_fusion
  43.2 1.4 %collective-permute-start.10 = (f32[2,1,16,128]{3,2,1,0:T(8,128)S(1)}, f32[2,1,16,128]{3,2,1,0:T(8,128)S(1)}, u32[]{:S(2)}, u32[]{:S(2)}) collective-permute-start(f32[2,1,16,128]{3,2,1,0:T(8,128)S(1)} %get-tuple-element.29), channel_id=1, source_target_pairs={{0,4},{4,0},{8,12},{12,8},{16,20},{20,16},{24,28},{28,24},{1,5},{5... | collective-permute-start | bytes 49160 | tf_op jit(solution)/shard_map/ppermute | solution.py:32
  44.7 1.6 %collective-permute-start.11 = (f32[2,1,16,128]{3,2,1,0:T(8,128)S(1)}, f32[2,1,16,128]{3,2,1,0:T(8,128)S(1)}, u32[]{:S(2)}, u32[]{:S(2)}) collective-permute-start(f32[2,1,16,128]{3,2,1,0:T(8,128)S(1)} %get-tuple-element.30), channel_id=1, source_target_pairs={{0,6},{1,7},{2,4},{3,5},{4,2},{5,3},{6,0},{7,1},{8,14},{9,15},{10,... | collective-permute-start | bytes 49160 | tf_op jit(solution)/shard_map/ppermute | solution.py:43
  46.2 0.5 collective-permute-start.9
  46.8 0.2 collective-permute-done.10
  47.0 2.3 %collective-permute-done.11 = f32[2,1,16,128]{3,2,1,0:T(8,128)S(1)} collective-permute-done((f32[2,1,16,128]{3,2,1,0:T(8,128)S(1)}, f32[2,1,16,128]{3,2,1,0:T(8,128)S(1)}, u32[]{:S(2)}, u32[]{:S(2)}) %collective-permute-start.11) | collective-permute-done | bytes 16416 | tf_op jit(solution)/shard_map/ppermute | solution.py:43
  49.3 0.6 %collective-permute-done.9 = f32[2,1,16,128]{3,2,1,0:T(8,128)S(1)} collective-permute-done((f32[2,1,16,128]{3,2,1,0:T(8,128)S(1)}, f32[2,1,16,128]{3,2,1,0:T(8,128)S(1)}, u32[]{:S(2)}, u32[]{:S(2)}) %collective-permute-start.9) | collective-permute-done | bytes 16416 | tf_op jit(solution)/shard_map/ppermute | solution.py:32
  50.0 0.1 add_select_fusion.1.refs_0_
  50.0 2.7 %collective-permute-start.12 = (f32[2,1,16,128]{3,2,1,0:T(8,128)S(1)}, f32[2,1,16,128]{3,2,1,0:T(8,128)S(1)}, u32[]{:S(2)}, u32[]{:S(2)}) collective-permute-start(f32[2,1,16,128]{3,2,1,0:T(8,128)S(1)} %add_select_fusion.1.refs_0_), channel_id=1, source_target_pairs={{0,24},{4,28},{8,16},{12,20},{16,8},{20,12},{24,0},{28,4},{1,25},{... | collective-permute-start | bytes 49160 | tf_op jit(solution)/shard_map/ppermute | solution.py:32
  52.7 0.0 collective-permute-start.13
  52.7 1.7 %collective-permute-start.14 = (f32[2,1,16,128]{3,2,1,0:T(8,128)S(1)}, f32[2,1,16,128]{3,2,1,0:T(8,128)S(1)}, u32[]{:S(2)}, u32[]{:S(2)}) collective-permute-start(f32[2,1,16,128]{3,2,1,0:T(8,128)S(1)} %add_select_fusion.1.refs_0_), channel_id=1, source_target_pairs={{0,16},{4,20},{8,24},{12,28},{16,0},{20,4},{24,8},{28,12},{1,17},{... | collective-permute-start | bytes 49160 | tf_op jit(solution)/shard_map/ppermute | solution.py:32
  54.4 1.1 %collective-permute-done.12.refs_1_ = f32[2,1,16,128]{3,2,1,0:T(8,128)S(1)} collective-permute-done((f32[2,1,16,128]{3,2,1,0:T(8,128)S(1)}, f32[2,1,16,128]{3,2,1,0:T(8,128)S(1)}, u32[]{:S(2)}, u32[]{:S(2)}) %collective-permute-start.12) | collective-permute-done | bytes 16416 | tf_op jit(solution)/shard_map/ppermute | solution.py:32
  55.6 0.9 %collective-permute-done.13.refs_2_ = f32[2,1,16,128]{3,2,1,0:T(8,128)S(1)} collective-permute-done((f32[2,1,16,128]{3,2,1,0:T(8,128)S(1)}, f32[2,1,16,128]{3,2,1,0:T(8,128)S(1)}, u32[]{:S(2)}, u32[]{:S(2)}) %collective-permute-start.13) | collective-permute-done | bytes 16416 | tf_op jit(solution)/shard_map/ppermute | solution.py:32
  56.5 0.9 %collective-permute-done.14.refs_3_ = f32[2,1,16,128]{3,2,1,0:T(8,128)S(1)} collective-permute-done((f32[2,1,16,128]{3,2,1,0:T(8,128)S(1)}, f32[2,1,16,128]{3,2,1,0:T(8,128)S(1)}, u32[]{:S(2)}, u32[]{:S(2)}) %collective-permute-start.14) | collective-permute-done | bytes 16416 | tf_op jit(solution)/shard_map/ppermute | solution.py:32
  57.4 0.8 %finish.1 = (f32[1,16]{1,0:T(1,128)}, f32[1,16]{1,0:T(1,128)}, f32[16,128]{1,0:T(8,128)}) custom-call(s32[16,128]{1,0:T(8,128)S(1)} %get-tuple-element.17.keep_rows_ref, f32[2,1,16,128]{3,2,1,0:T(8,128)S(1)} %add_select_fusion.1.refs_0_, f32[2,1,16,128]{3,2,1,0:T(8,128)S(1)} %collective-permute-done.12.refs_1_, ...), custom_call_target="tpu_custom_call" | custom-call | tf_op jit(solution)/shard_map/finish/pallas_call | solution.py:394
  (17 shorter events, 0.1 us)
Async XLA Ops:
  0.6 10.4 %copy-start.5 = (bf16[16,1024]{1,0:T(8,128)(2,1)S(1)}, bf16[16,1024]{1,0:T(8,128)(2,1)}, u32[]{:S(2)}) copy-start(bf16[16,1024]{1,0:T(8,128)(2,1)} %param.7) | copy-start | bytes 98308
  0.6 10.5 %collective-permute-start = (bf16[1,16,1024]{2,1,0:T(8,128)(2,1)}, bf16[1,16,1024]{2,1,0:T(8,128)(2,1)S(1)}, u32[]{:S(2)}, u32[]{:S(2)}) collective-permute-start(bf16[1,16,1024]{2,1,0:T(8,128)(2,1)} %bitcast.6), channel_id=1, source_target_pairs={{0,16},{4,20},{8,24},{12,28},{16,0},{20,4},{24,8},{28,12},{1,17},{... | collective-permute-start | bytes 98312 | tf_op jit(solution)/shard_map/ppermute | solution.py:32
  4.8 6.3 %collective-permute-start.1 = (bf16[1,16,1024]{2,1,0:T(8,128)(2,1)}, bf16[1,16,1024]{2,1,0:T(8,128)(2,1)S(1)}, u32[]{:S(2)}, u32[]{:S(2)}) collective-permute-start(bf16[1,16,1024]{2,1,0:T(8,128)(2,1)} %bitcast.7), channel_id=1, source_target_pairs={{0,8},{4,12},{8,0},{12,4},{16,24},{20,28},{24,16},{28,20},{1,9},{5... | collective-permute-start | bytes 98312 | tf_op jit(solution)/shard_map/ppermute | solution.py:32
  6.3 5.9 %collective-permute-start.2 = (bf16[1,16,1024]{2,1,0:T(8,128)(2,1)}, bf16[1,16,1024]{2,1,0:T(8,128)(2,1)S(1)}, u32[]{:S(2)}, u32[]{:S(2)}) collective-permute-start(bf16[1,16,1024]{2,1,0:T(8,128)(2,1)} %bitcast.8), channel_id=1, source_target_pairs={{0,24},{4,28},{8,16},{12,20},{16,8},{20,12},{24,0},{28,4},{1,25},{... | collective-permute-start | bytes 98312 | tf_op jit(solution)/shard_map/ppermute | solution.py:32
  12.3 5.2 %copy-start = (bf16[8192]{0:T(1024)(128)(2,1)S(1)}, bf16[8192]{0:T(1024)(128)(2,1)}, u32[]{:S(2)}) copy-start(bf16[8192]{0:T(1024)(128)(2,1)} %gain_ref.1) | copy-start | bytes 49156
  12.3 7.5 %copy-start.1 = (s32[64,128]{1,0:T(8,128)S(1)}, s32[64,128]{1,0:T(8,128)}, u32[]{:S(2)}) copy-start(s32[64,128]{1,0:T(8,128)} %param.12) | copy-start | bytes 98308
  12.3 7.5 %copy-start.2 = (f32[16]{0:T(128)S(1)}, f32[16]{0:T(128)}, u32[]{:S(2)}) copy-start(f32[16]{0:T(128)} %heat_ref.1) | copy-start | bytes 196
  12.3 7.5 %copy-start.3 = (s32[64]{0:T(128)S(1)}, s32[64]{0:T(128)}, u32[]{:S(2)}) copy-start(s32[64]{0:T(128)} %choice_ref.1) | copy-start | bytes 772
  12.3 7.5 %copy-start.4 = (s32[64]{0:T(128)S(1)}, s32[64]{0:T(128)}, u32[]{:S(2)}) copy-start(s32[64]{0:T(128)} %keep_ref.1) | copy-start | bytes 772
  12.4 5.1 %collective-permute-start.3 = (bf16[4,16,1024]{2,1,0:T(8,128)(2,1)S(1)}, bf16[4,16,1024]{2,1,0:T(8,128)(2,1)S(1)}, u32[]{:S(2)}, u32[]{:S(2)}) collective-permute-start(bf16[4,16,1024]{2,1,0:T(8,128)(2,1)S(1)} %pad_maximum_fusion.3.refs_0_), channel_id=1, source_target_pairs={{0,4},{4,0},{8,12},{12,8},{16,20},{20,16},{24,28},{28,24},{1,5},{5... | collective-permute-start | bytes 393224 | tf_op jit(solution)/shard_map/ppermute | solution.py:32
  17.7 6.8 %collective-permute-start.6 = (bf16[1,16,4096]{2,1,0:T(8,128)(2,1)S(1)}, bf16[1,16,4096]{2,1,0:T(8,128)(2,1)S(1)}, u32[]{:S(2)}, u32[]{:S(2)}) collective-permute-start(bf16[1,16,4096]{2,1,0:T(8,128)(2,1)S(1)} %get-tuple-element.16.after_ref), channel_id=1, source_target_pairs={{0,2},{1,3},{2,0},{3,1},{4,6},{5,7},{6,4},{7,5},{8,10},{9,11},{10,... | collective-permute-start | bytes 393224 | tf_op jit(solution)/shard_map/ppermute | solution.py:32
  19.3 7.0 %collective-permute-start.4 = (bf16[1,16,4096]{2,1,0:T(8,128)(2,1)S(1)}, bf16[1,16,4096]{2,1,0:T(8,128)(2,1)S(1)}, u32[]{:S(2)}, u32[]{:S(2)}) collective-permute-start(bf16[1,16,4096]{2,1,0:T(8,128)(2,1)S(1)} %get-tuple-element.18), channel_id=1, source_target_pairs={{0,2},{1,3},{2,0},{3,1},{4,6},{5,7},{6,4},{7,5},{8,10},{9,11},{10,... | collective-permute-start | bytes 393224 | tf_op jit(solution)/shard_map/ppermute | solution.py:32
  24.5 2.3 %collective-permute-start.7 = (bf16[2,16,4096]{2,1,0:T(8,128)(2,1)S(1)}, bf16[2,16,4096]{2,1,0:T(8,128)(2,1)S(1)}, u32[]{:S(2)}, u32[]{:S(2)}) collective-permute-start(bf16[2,16,4096]{2,1,0:T(8,128)(2,1)S(1)} %constant_dynamic-update-slice_fusion.5.refs_0_), channel_id=1, source_target_pairs={{0,1},{1,0},{2,3},{3,2},{4,5},{5,4},{6,7},{7,6},{8,9},{9,8},{10,11... | collective-permute-start | bytes 786440 | tf_op jit(solution)/shard_map/ppermute | solution.py:32
  26.3 6.7 %collective-permute-start.5 = (bf16[2,16,4096]{2,1,0:T(8,128)(2,1)S(1)}, bf16[2,16,4096]{2,1,0:T(8,128)(2,1)S(1)}, u32[]{:S(2)}, u32[]{:S(2)}) collective-permute-start(bf16[2,16,4096]{2,1,0:T(8,128)(2,1)S(1)} %pad_maximum_fusion.2), channel_id=1, source_target_pairs={{0,1},{1,0},{2,3},{3,2},{4,5},{5,4},{6,7},{7,6},{8,9},{9,8},{10,11... | collective-permute-start | bytes 786440 | tf_op jit(solution)/shard_map/ppermute | solution.py:32
  41.9 1.3 %collective-permute-start.8 = (f32[2,2,16,128]{3,2,1,0:T(8,128)S(1)}, f32[2,2,16,128]{3,2,1,0:T(8,128)S(1)}, u32[]{:S(2)}, u32[]{:S(2)}) collective-permute-start(f32[2,2,16,128]{3,2,1,0:T(8,128)S(1)} %get-tuple-element.25), channel_id=1, source_target_pairs={{0,1},{1,0},{2,3},{3,2},{4,5},{5,4},{6,7},{7,6},{8,9},{9,8},{10,11... | collective-permute-start | bytes 98312 | tf_op jit(solution)/shard_map/ppermute | solution.py:32
  43.2 3.8 %collective-permute-start.10 = (f32[2,1,16,128]{3,2,1,0:T(8,128)S(1)}, f32[2,1,16,128]{3,2,1,0:T(8,128)S(1)}, u32[]{:S(2)}, u32[]{:S(2)}) collective-permute-start(f32[2,1,16,128]{3,2,1,0:T(8,128)S(1)} %get-tuple-element.29), channel_id=1, source_target_pairs={{0,4},{4,0},{8,12},{12,8},{16,20},{20,16},{24,28},{28,24},{1,5},{5... | collective-permute-start | bytes 49160 | tf_op jit(solution)/shard_map/ppermute | solution.py:32
  44.7 4.7 %collective-permute-start.11 = (f32[2,1,16,128]{3,2,1,0:T(8,128)S(1)}, f32[2,1,16,128]{3,2,1,0:T(8,128)S(1)}, u32[]{:S(2)}, u32[]{:S(2)}) collective-permute-start(f32[2,1,16,128]{3,2,1,0:T(8,128)S(1)} %get-tuple-element.30), channel_id=1, source_target_pairs={{0,6},{1,7},{2,4},{3,5},{4,2},{5,3},{6,0},{7,1},{8,14},{9,15},{10,... | collective-permute-start | bytes 49160 | tf_op jit(solution)/shard_map/ppermute | solution.py:43
  46.2 3.7 %collective-permute-start.9 = (f32[2,1,16,128]{3,2,1,0:T(8,128)S(1)}, f32[2,1,16,128]{3,2,1,0:T(8,128)S(1)}, u32[]{:S(2)}, u32[]{:S(2)}) collective-permute-start(f32[2,1,16,128]{3,2,1,0:T(8,128)S(1)} %get-tuple-element.30), channel_id=1, source_target_pairs={{0,2},{1,3},{2,0},{3,1},{4,6},{5,7},{6,4},{7,5},{8,10},{9,11},{10,... | collective-permute-start | bytes 49160 | tf_op jit(solution)/shard_map/ppermute | solution.py:32
  50.0 5.6 %collective-permute-start.12 = (f32[2,1,16,128]{3,2,1,0:T(8,128)S(1)}, f32[2,1,16,128]{3,2,1,0:T(8,128)S(1)}, u32[]{:S(2)}, u32[]{:S(2)}) collective-permute-start(f32[2,1,16,128]{3,2,1,0:T(8,128)S(1)} %add_select_fusion.1.refs_0_), channel_id=1, source_target_pairs={{0,24},{4,28},{8,16},{12,20},{16,8},{20,12},{24,0},{28,4},{1,25},{... | collective-permute-start | bytes 49160 | tf_op jit(solution)/shard_map/ppermute | solution.py:32
  52.7 3.7 %collective-permute-start.13 = (f32[2,1,16,128]{3,2,1,0:T(8,128)S(1)}, f32[2,1,16,128]{3,2,1,0:T(8,128)S(1)}, u32[]{:S(2)}, u32[]{:S(2)}) collective-permute-start(f32[2,1,16,128]{3,2,1,0:T(8,128)S(1)} %add_select_fusion.1.refs_0_), channel_id=1, source_target_pairs={{0,8},{4,12},{8,0},{12,4},{16,24},{20,28},{24,16},{28,20},{1,9},{5... | collective-permute-start | bytes 49160 | tf_op jit(solution)/shard_map/ppermute | solution.py:32
  52.7 4.6 %collective-permute-start.14 = (f32[2,1,16,128]{3,2,1,0:T(8,128)S(1)}, f32[2,1,16,128]{3,2,1,0:T(8,128)S(1)}, u32[]{:S(2)}, u32[]{:S(2)}) collective-permute-start(f32[2,1,16,128]{3,2,1,0:T(8,128)S(1)} %add_select_fusion.1.refs_0_), channel_id=1, source_target_pairs={{0,16},{4,20},{8,24},{12,28},{16,0},{20,4},{24,8},{28,12},{1,17},{... | collective-permute-start | bytes 49160 | tf_op jit(solution)/shard_map/ppermute | solution.py:32
